TPU v7x, 32 devices: a whole 2x2x4 slice. The times are simulated.
32 devices in a mesh: dp: 8 (over y, x, core), mp: 4 (over z).
Axes of the slice: x: 2, y: 2, z: 4, core: 2. Of those that a mesh axis runs over, the one named last changes fastest.
Arguments:
- hidden: bfloat16 [8192, 2048], P('dp'), may hold values from -6 to 6
- cotangent: bfloat16 [8192, 2048], P('dp'), may hold values from -6 to 6
- lengths: int32 [16], P('dp'), may hold values from 64 to 512, as said below
- input_gain: bfloat16 [2048], P('dp'), may hold values from 0.5 to 1.5
- input_shift: bfloat16 [2048], P('dp'), may hold values from -1.25 to 1.25
- triple_weight: bfloat16 [2048, 3, 2048], P('dp', None, 'mp'), may hold values from -0.125 to 0.125
- triple_bias: bfloat16 [2, 2048], P(None, 'mp'), may hold values from -1.25 to 1.25
- merge_weight: bfloat16 [2048, 2048], P('mp', 'dp'), may hold values from -0.5 to 0.5
- merge_bias: bfloat16 [2048], P('dp'), may hold values from -1.25 to 1.25
- middle_gain: bfloat16 [2048], P('dp'), may hold values from 0.5 to 1.5
- middle_shift: bfloat16 [2048], P('dp'), may hold values from -1.25 to 1.25
- expand_weight: bfloat16 [2048, 8192], P('dp', 'mp'), may hold values from -0.125 to 0.125
- expand_bias: bfloat16 [8192], P('mp'), may hold values from -1.25 to 1.25
- reduce_weight: bfloat16 [8192, 2048], P('mp', 'dp'), may hold values from -0.0625 to 0.0625
- reduce_bias: bfloat16 [2048], P('dp'), may hold values from -1.25 to 1.25
Outputs:
- layer_output: bfloat16 [8192, 2048], P('dp')
- hidden_grad: bfloat16 [8192, 2048], P('dp')
- input_gain_grad: float32 [2048], P('dp')
- input_shift_grad: float32 [2048], P('dp')
- triple_weight_grad: float32 [2048, 3, 2048], P('dp', None, 'mp')
- triple_bias_grad: float32 [2, 2048], P(None, 'mp')
- merge_weight_grad: float32 [2048, 2048], P('mp', 'dp')
- merge_bias_grad: float32 [2048], P('dp')
- middle_gain_grad: float32 [2048], P('dp')
- middle_shift_grad: float32 [2048], P('dp')
- expand_weight_grad: float32 [2048, 8192], P('dp', 'mp')
- expand_bias_grad: float32 [8192], P('mp')
- reduce_weight_grad: float32 [8192, 2048], P('mp', 'dp')
- reduce_bias_grad: float32 [2048], P('dp')
- branch_rms: float32 [3], replicated
Inputs may be any that keep to these rules, and one draw needn't show every extreme that they name: `lengths`: each slot's valid tokens stand at its start; in every draw some slot is full (512 valid tokens).
All inputs are finite; a program needn't handle non-finite values.
Results may differ from a plain program's by a relative error of at most 0.023.
Values may be sent and summed in bfloat16 or wider, within the bound.
A program may use at most 256 MiB of HBM per device.

v0:
```python
import jax
import jax.numpy as jnp
from jax import lax
from jax.sharding import PartitionSpec as P

HEADS = 32
HEAD_DIM = 64
SLOT = 512
MICRO = 2


def layer_norm(values, gain_vec, shift_vec):
    center = values - jnp.mean(values, axis=-1, keepdims=True)
    spread = jnp.mean(center * center, axis=-1, keepdims=True)
    return center * lax.rsqrt(spread + 1e-05) * gain_vec + shift_vec


def gelu_exact(values):
    return jax.nn.gelu(values, approximate=False)


def attention_scores(query_low, key_low, slopes, length):
    raw_scores = jnp.einsum("qhe,khe->hqk", query_low, key_low, preferred_element_type=jnp.float32)
    places = jnp.arange(query_low.shape[0], dtype=jnp.int32)
    key_place = places.astype(jnp.float32)
    scores = (raw_scores + slopes[:, None, None] * key_place[None, None, :]) * 0.125
    allowed = (places[None, :] <= places[:, None]) & (places[None, :] < length)
    return jnp.where(allowed[None], scores, -1000000000.0)


def local(
    hidden,
    cotangent,
    lengths,
    input_gain,
    input_shift,
    triple_weight,
    triple_bias,
    merge_weight,
    merge_bias,
    middle_gain,
    middle_shift,
    expand_weight,
    expand_bias,
    reduce_weight,
    reduce_bias,
):
    slot = SLOT
    width = hidden.shape[1]
    head_cols = triple_weight.shape[2]
    unit_cols = expand_weight.shape[1]
    local_heads = head_cols // HEAD_DIM
    head_start = lax.axis_index("mp") * local_heads
    slopes = 2.0 ** (
        -8.0
        * (head_start + jnp.arange(local_heads, dtype=jnp.int32) + 1).astype(jnp.float32)
        / HEADS
    )
    bias_pair = triple_bias.astype(jnp.float32)
    unit_shift = expand_bias.astype(jnp.float32)
    attention_kept = (
        lax.all_gather(input_gain, "dp", axis=0, tiled=True),
        lax.all_gather(input_shift, "dp", axis=0, tiled=True),
        lax.all_gather(triple_weight, "dp", axis=0, tiled=True),
        lax.all_gather(merge_weight, "dp", axis=1, tiled=True),
        lax.all_gather(merge_bias, "dp", axis=0, tiled=True),
    )
    feed_kept = (
        lax.all_gather(middle_gain, "dp", axis=0, tiled=True),
        lax.all_gather(middle_shift, "dp", axis=0, tiled=True),
        lax.all_gather(expand_weight, "dp", axis=0, tiled=True),
        lax.all_gather(reduce_weight, "dp", axis=1, tiled=True),
        lax.all_gather(reduce_bias, "dp", axis=0, tiled=True),
    )
    acc_triple = jnp.zeros((width, 3, head_cols), jnp.float32)
    acc_merge = jnp.zeros((head_cols, width), jnp.float32)
    acc_expand = jnp.zeros((width, unit_cols), jnp.float32)
    acc_reduce = jnp.zeros((unit_cols, width), jnp.float32)
    acc_gain_one = jnp.zeros((width,), jnp.float32)
    acc_shift_one = jnp.zeros((width,), jnp.float32)
    acc_merge_bias = jnp.zeros((width,), jnp.float32)
    acc_gain_two = jnp.zeros((width,), jnp.float32)
    acc_shift_two = jnp.zeros((width,), jnp.float32)
    acc_reduce_bias = jnp.zeros((width,), jnp.float32)
    acc_pair_bias = jnp.zeros((2, head_cols), jnp.float32)
    acc_unit_bias = jnp.zeros((unit_cols,), jnp.float32)
    square_sums = jnp.zeros((4,), jnp.float32)
    output_parts = []
    grad_parts = []
    for batch_index in range(MICRO):
        start = batch_index * slot
        token_rows = hidden[start : start + slot].astype(jnp.float32)
        length = lengths[batch_index]
        valid_rows = (jnp.arange(slot, dtype=jnp.int32) < length)[:, None]
        gain_one, shift_one, triple_full, merge_full, merge_shift = attention_kept
        gain_two, shift_two, expand_full, reduce_full, reduce_shift = feed_kept
        gain_one = gain_one.astype(jnp.float32)
        shift_one = shift_one.astype(jnp.float32)
        gain_two = gain_two.astype(jnp.float32)
        shift_two = shift_two.astype(jnp.float32)
        norm_in = layer_norm(token_rows, gain_one, shift_one).astype(jnp.bfloat16)
        triple = jnp.einsum("td,dcf->tcf", norm_in, triple_full, preferred_element_type=jnp.float32)
        query_low = (
            (triple[:, 0] + bias_pair[0]).astype(jnp.bfloat16).reshape(slot, local_heads, HEAD_DIM)
        )
        key_low = triple[:, 1].astype(jnp.bfloat16).reshape(slot, local_heads, HEAD_DIM)
        value_low = (
            (triple[:, 2] + bias_pair[1]).astype(jnp.bfloat16).reshape(slot, local_heads, HEAD_DIM)
        )
        scores = attention_scores(query_low, key_low, slopes, length)
        log_total = jax.nn.logsumexp(scores, axis=-1)
        attention_weights = jnp.exp(scores - log_total[..., None]).astype(jnp.bfloat16)
        mixed_heads = jnp.einsum(
            "hqk,khe->qhe", attention_weights, value_low, preferred_element_type=jnp.float32
        )
        mixed_heads = mixed_heads.reshape(slot, head_cols).astype(jnp.bfloat16)
        attention_part = jnp.dot(mixed_heads, merge_full, preferred_element_type=jnp.float32)
        attention_branch = lax.psum(attention_part.astype(jnp.bfloat16), "mp").astype(
            jnp.float32
        ) + merge_shift.astype(jnp.float32)
        residual = token_rows + attention_branch
        norm_mid = layer_norm(residual, gain_two, shift_two).astype(jnp.bfloat16)
        token_count = length.astype(jnp.float32)
        expand_pre = jnp.dot(norm_mid, expand_full, preferred_element_type=jnp.float32) + unit_shift
        activation = gelu_exact(expand_pre).astype(jnp.bfloat16)
        feed_part = jnp.dot(activation, reduce_full, preferred_element_type=jnp.float32)
        feed_branch = lax.psum(feed_part.astype(jnp.bfloat16), "mp").astype(
            jnp.float32
        ) + reduce_shift.astype(jnp.float32)
        result = residual + feed_branch
        output_parts.append(jnp.where(valid_rows, result, 0.0).astype(jnp.bfloat16))
        square_sums = square_sums + jnp.stack(
            [
                jnp.sum(jnp.where(valid_rows, result * result, 0.0)),
                jnp.sum(jnp.where(valid_rows, attention_branch * attention_branch, 0.0)),
                jnp.sum(jnp.where(valid_rows, feed_branch * feed_branch, 0.0)),
                token_count,
            ]
        )
        grad_out = jnp.where(valid_rows, cotangent[start : start + slot].astype(jnp.float32), 0.0)
        grad_feed = grad_out.astype(jnp.bfloat16)
        acc_reduce_bias = acc_reduce_bias + jnp.sum(grad_out, axis=0)
        acc_reduce = acc_reduce + jnp.dot(
            activation.T, grad_feed, preferred_element_type=jnp.float32
        )
        grad_act = jnp.dot(grad_feed, reduce_full.T, preferred_element_type=jnp.float32)
        gelu_value, gelu_back = jax.vjp(gelu_exact, expand_pre)
        grad_pre = gelu_back(grad_act)[0].astype(jnp.bfloat16)
        acc_unit_bias = acc_unit_bias + jnp.sum(grad_pre, axis=0, dtype=jnp.float32)
        acc_expand = acc_expand + jnp.dot(norm_mid.T, grad_pre, preferred_element_type=jnp.float32)
        mid_part = jnp.dot(grad_pre, expand_full.T, preferred_element_type=jnp.float32)
        grad_mid = lax.psum(mid_part.astype(jnp.bfloat16), "mp").astype(jnp.float32)
        norm_value, norm_back = jax.vjp(layer_norm, residual, gain_two, shift_two)
        grad_resid_norm, grad_gain_two, grad_shift_two = norm_back(grad_mid)
        acc_gain_two = acc_gain_two + grad_gain_two
        acc_shift_two = acc_shift_two + grad_shift_two
        grad_residual = grad_out + grad_resid_norm
        grad_branch = grad_residual.astype(jnp.bfloat16)
        acc_merge_bias = acc_merge_bias + jnp.sum(grad_branch, axis=0, dtype=jnp.float32)
        acc_merge = acc_merge + jnp.dot(
            mixed_heads.T, grad_branch, preferred_element_type=jnp.float32
        )
        grad_mixed = jnp.dot(grad_branch, merge_full.T, preferred_element_type=jnp.float32)
        grad_mixed = grad_mixed.astype(jnp.bfloat16).reshape(slot, local_heads, HEAD_DIM)
        again_scores = attention_scores(query_low, key_low, slopes, length)
        soft_weights = jnp.exp(again_scores - log_total[..., None])
        grad_probs = jnp.einsum(
            "qhe,khe->hqk", grad_mixed, value_low, preferred_element_type=jnp.float32
        )
        grad_value = jnp.einsum(
            "hqk,qhe->khe",
            soft_weights.astype(jnp.bfloat16),
            grad_mixed,
            preferred_element_type=jnp.float32,
        ).astype(jnp.bfloat16)
        row_terms = jnp.sum(soft_weights * grad_probs, axis=-1, keepdims=True)
        grad_scores = (soft_weights * (grad_probs - row_terms)).astype(jnp.bfloat16)
        grad_query = (
            0.125
            * jnp.einsum("hqk,khe->qhe", grad_scores, key_low, preferred_element_type=jnp.float32)
        ).astype(jnp.bfloat16)
        grad_key = (
            0.125
            * jnp.einsum("hqk,qhe->khe", grad_scores, query_low, preferred_element_type=jnp.float32)
        ).astype(jnp.bfloat16)
        grad_triple = jnp.stack([grad_query, grad_key, grad_value], axis=1).reshape(
            slot, 3, head_cols
        )
        acc_pair_bias = acc_pair_bias + jnp.stack(
            [
                jnp.sum(grad_triple[:, 0], axis=0, dtype=jnp.float32),
                jnp.sum(grad_triple[:, 2], axis=0, dtype=jnp.float32),
            ]
        )
        acc_triple = acc_triple + jnp.einsum(
            "td,tcf->dcf", norm_in, grad_triple, preferred_element_type=jnp.float32
        )
        grad_in_part = jnp.einsum(
            "tcf,dcf->td", grad_triple, triple_full, preferred_element_type=jnp.float32
        )
        grad_in = lax.psum(grad_in_part.astype(jnp.bfloat16), "mp").astype(jnp.float32)
        first_value, first_back = jax.vjp(layer_norm, token_rows, gain_one, shift_one)
        grad_rows_norm, grad_gain_one, grad_shift_one = first_back(grad_in)
        acc_gain_one = acc_gain_one + grad_gain_one
        acc_shift_one = acc_shift_one + grad_shift_one
        input_rows_grad = (grad_residual + grad_rows_norm).astype(jnp.bfloat16)
        grad_parts.append(input_rows_grad)
    owned = (
        lax.psum_scatter(
            acc_triple.astype(jnp.bfloat16), "dp", scatter_dimension=0, tiled=True
        ).astype(jnp.float32),
        lax.psum_scatter(
            acc_merge.astype(jnp.bfloat16), "dp", scatter_dimension=1, tiled=True
        ).astype(jnp.float32),
        lax.psum_scatter(
            acc_expand.astype(jnp.bfloat16), "dp", scatter_dimension=0, tiled=True
        ).astype(jnp.float32),
        lax.psum_scatter(
            acc_reduce.astype(jnp.bfloat16), "dp", scatter_dimension=1, tiled=True
        ).astype(jnp.float32),
        lax.psum_scatter(
            acc_gain_one.astype(jnp.bfloat16), "dp", scatter_dimension=0, tiled=True
        ).astype(jnp.float32),
        lax.psum_scatter(
            acc_shift_one.astype(jnp.bfloat16), "dp", scatter_dimension=0, tiled=True
        ).astype(jnp.float32),
        lax.psum_scatter(
            acc_merge_bias.astype(jnp.bfloat16), "dp", scatter_dimension=0, tiled=True
        ).astype(jnp.float32),
        lax.psum_scatter(
            acc_gain_two.astype(jnp.bfloat16), "dp", scatter_dimension=0, tiled=True
        ).astype(jnp.float32),
        lax.psum_scatter(
            acc_shift_two.astype(jnp.bfloat16), "dp", scatter_dimension=0, tiled=True
        ).astype(jnp.float32),
        lax.psum_scatter(
            acc_reduce_bias.astype(jnp.bfloat16), "dp", scatter_dimension=0, tiled=True
        ).astype(jnp.float32),
    )
    pair_grad, unit_grad, total_sums = lax.psum((acc_pair_bias, acc_unit_bias, square_sums), "dp")
    root_means = jnp.sqrt(total_sums[:3] / (total_sums[3] * width))
    layer_output = jnp.concatenate(output_parts, axis=0)
    hidden_grad = jnp.concatenate(grad_parts, axis=0)
    return (
        layer_output,
        hidden_grad,
        owned[4],
        owned[5],
        owned[0],
        pair_grad,
        owned[1],
        owned[6],
        owned[7],
        owned[8],
        owned[2],
        unit_grad,
        owned[3],
        owned[9],
        root_means,
    )


def solution(mesh):
    return jax.shard_map(
        local,
        mesh=mesh,
        in_specs=(
            P("dp", None),
            P("dp", None),
            P("dp"),
            P("dp"),
            P("dp"),
            P("dp", None, "mp"),
            P(None, "mp"),
            P("mp", "dp"),
            P("dp"),
            P("dp"),
            P("dp"),
            P("dp", "mp"),
            P("mp"),
            P("mp", "dp"),
            P("dp"),
        ),
        out_specs=(
            P("dp", None),
            P("dp", None),
            P("dp"),
            P("dp"),
            P("dp", None, "mp"),
            P(None, "mp"),
            P("mp", "dp"),
            P("dp"),
            P("dp"),
            P("dp"),
            P("dp", "mp"),
            P("mp"),
            P("mp", "dp"),
            P("dp"),
            P(),
        ),
        check_vma=False,
    )
```

profile of v0, /device:TPU:0, one launch (start us, length us, event | category | flops | bytes accessed | tf_op | source)
XLA Modules:
  0.0 1231.0 jit_solution(12049603003931523445)
XLA Ops:
  17.5 10.6 all-gather
  28.1 8.9 all-gather.1
  37.4 22.4 %all-gather.11.cloned.1.call-done = bf16[2048,3,512]{0,2,1:T(8,128)(2,1)} async-done(((bf16[256,3,512]{0,2,1:T(8,128)(2,1)}), bf16[2048,3,512]{0,2,1:T(8,128)(2,1)}) %all-gather.11.cloned.1.call-update) | async-done | bytes 6291472 | tf_op jit(solution)/shard_map/all_gather | solution.py:64
  73.6 16.2 %all-gather.13.cloned.1.call-done = bf16[512,2048]{1,0:T(8,128)(2,1)} async-done(((bf16[512,256]{1,0:T(8,128)(2,1)}), bf16[512,2048]{1,0:T(8,128)(2,1)}) %all-gather.13.cloned.1.call-update) | async-done | bytes 2097168 | tf_op jit(solution)/shard_map/all_gather | solution.py:65
  94.1 9.3 all-gather.2
  104.3 76.0 %all-reduce.15.cloned.1.call-done = bf16[512,2048]{1,0:T(8,128)(2,1)} async-done(((bf16[512,2048]{1,0:T(8,128)(2,1)}), bf16[512,2048]{1,0:T(8,128)(2,1)}) %all-reduce.15.cloned.1.call-update) | async-done | bytes 2097168 | tf_op jit(solution)/shard_map/psum | solution.py:118
  203.0 8.9 all-gather.3
  212.0 9.1 all-gather.4
  221.1 66.0 %all-reduce.17.cloned.1.call-done = bf16[512,2048]{1,0:T(8,128)(2,1)} async-done(((bf16[512,2048]{1,0:T(8,128)(2,1)}), bf16[512,2048]{1,0:T(8,128)(2,1)}) %all-reduce.17.cloned.1.call-update) | async-done | bytes 2097168 | tf_op jit(solution)/shard_map/psum | solution.py:118
  293.0 49.2 %all-gather.15.cloned.1.call-done = bf16[2048,2048]{1,0:T(8,128)(2,1)} async-done(((bf16[256,2048]{1,0:T(8,128)(2,1)}), bf16[2048,2048]{1,0:T(8,128)(2,1)}) %all-gather.15.cloned.1.call-update) | async-done | bytes 8388624 | tf_op jit(solution)/shard_map/all_gather | solution.py:71
  353.0 26.4 %multiply_convert_fusion.3 = (bf16[512,2048]{1,0:T(8,128)(2,1)}, f32[512,2048]{1,0:T(8,128)}, bf16[512,2048]{1,0:T(8,128)(2,1)}, f32[512,2048]{1,0:T(8,128)}, f32[512,2048]{1,0:T(8,128)}) fusion(f32[2048]{0:T(1024)S(1)} %convert_element_type.369, f32[512,2048]{1,0:T(8,128)S(1)} %fusion.108, bf16[2048,2048]{1,0:T(8,128)(2,1)S(1)} %copy-done.105, ...), kind=kOutput, calls=%fused_computation.120 | convolution fusion | flops 4442816512 | bytes 33591296 | tf_op jit(solution)/shard_map/dot_general | solution.py:124
  379.4 20.4 %all-gather.17.cloned.1.call-done = bf16[2048,2048]{1,0:T(8,128)(2,1)} async-done(((bf16[2048,256]{1,0:T(8,128)(2,1)}), bf16[2048,2048]{1,0:T(8,128)(2,1)}) %all-gather.17.cloned.1.call-update) | async-done | bytes 8388624 | tf_op jit(solution)/shard_map/all_gather | solution.py:72
  399.8 12.9 %convert_reduce_fusion.6 = (f32[2048]{0:T(1024)}, bf16[512,2048]{1,0:T(8,128)(2,1)S(1)}) fusion(f32[512,2048]{1,0:T(8,128)} %get-tuple-element.85, bf16[2048,2048]{1,0:T(8,128)(2,1)} %all-gather.17.cloned.1.call-done, pred[512]{0:T(512)(128)(4,1)S(1)} %iota_compare_fusion.1, bf16[1024,2048]{1,0:T(8,128)(2,1)} %param.16, f32[512,2048]{1,0:T(8,128)} %copy-done.120, ...), kind=kOutput, calls=%fused_computation.81 | convolution fusion | flops 4315936768 | bytes 20988416 | tf_op jit(solution)/shard_map/dot_general | solution.py:146
  412.7 9.9 convolution_convert_fusion
  422.6 11.5 convert_reduce_fusion.7
  434.1 10.0 convolution_convert_fusion.1
  444.1 9.5 convolution_convert_fusion.2
  460.0 8.9 all-gather.5
  468.9 281.5 %all-reduce.21.cloned.1.call-done = (bf16[512,2048]{1,0:T(8,128)(2,1)}, bf16[512,2048]{1,0:T(8,128)(2,1)}, bf16[512,2048]{1,0:T(8,128)(2,1)}, bf16[512,2048]{1,0:T(8,128)(2,1)}) async-done(((bf16[512,2048]{1,0:T(8,128)(2,1)}, bf16[512,2048]{1,0:T(8,128)(2,1)}, bf16[512,2048]{1,0:T(8,128)(2,1)}, bf16[512,2048]{1,0:T(8,128)(2,1)}), (bf16[512,2048]{1,0:T(8,128)(2,1)}, bf16[512,2048]{1,0:T(8,128)(2,1)}, ...) | async-done | bytes 8388624 | tf_op jit(solution)/shard_map/psum | solution.py:127
  750.5 14.7 %select_reduce_fusion.5 = (f32[]{:T(128)}, f32[512]{0:T(512)S(1)}, f32[512]{0:T(512)S(1)}, f32[]{:T(128)}, f32[]{:T(128)}, /*index=5*/f32[]{:T(128)}, f32[]{:T(1...) fusion(bf16[512,2048]{1,0:T(8,128)(2,1)} %get-tuple-element.67,, ...), kind=kLoop, calls=%fused_computation.80 | loop fusion | flops 55567360 | bytes 25224216 | tf_op jit(solution)/shard_map/reduce_sum | solution.py:134
  807.6 9.5 multiply_convert_fusion
  854.1 13.8 %fusion.106 = f32[2048,2048]{1,0:T(8,128)} fusion(bf16[512,2048]{1,0:T(8,128)(2,1)} %copy-done.119, f32[2048]{0:T(1024)S(1)} %bitcast.180, f32[2048]{0:T(1024)S(1)} %bitcast.161, f32[512]{0:T(512)S(1)} %copy-done.74, bf16[512,2048]{1,0:T(8,128)(2,1)} %all-reduce.15.cloned.1.call-done, f32[512]{0:T(512)S(1)} %broadcast_multiply_fusion.3, ...), kind=kOutput, calls=%fused_computation.249 | convolution fusion | flops 4304404480 | bytes 23097344 | tf_op jit(solution)/shard_map/dot_general | solution.py:150
  867.9 15.6 %add_convert_fusion.1 = bf16[2048,2048]{1,0:T(8,128)(2,1)} fusion(f32[2048,2048]{1,0:T(8,128)} %fusion.106, bf16[512,2048]{1,0:T(8,128)(2,1)} %copy-done.121, f32[512]{0:T(512)S(1)} %copy-done.72, f32[2048]{0:T(1024)S(1)} %bitcast.181, f32[2048]{0:T(1024)S(1)} %bitcast.162, bf16[512,2048]{1,0:T(8,128)(2,1)} %all-reduce.17.cloned.1.call-done, ...), kind=kOutput, calls=%fused_computation.1 | convolution fusion | flops 4312793088 | bytes 31485952 | tf_op jit(solution)/shard_map/dot_general | solution.py:150
  885.0 10.0 fusion.71
  895.0 11.0 add_convert_fusion
  907.4 8.8 fusion.70
  931.9 25.5 %all-reduce.6 = (f32[2,512]{1,0:T(2,128)}, f32[2048]{0:T(1024)}, f32[4]{0:T(128)S(1)}) all-reduce(f32[2,512]{1,0:T(2,128)S(1)} %maximum_add_fusion, f32[2048]{0:T(1024)S(1)} %add.360, f32[4]{0:T(128)S(1)} %maximum_add_fusion.1), channel_id=1, replica_groups=mesh['dp'=8,'mp'=4] {'dp'}, use_global_device_ids=true, to_apply=%region_41.42 | all-reduce | flops 3076 | bytes 24608 | tf_op jit(solution)/shard_map/psum | solution.py:240
  965.2 42.5 %all-reduce.19.cloned.1.call-done = (bf16[512,2048]{1,0:T(8,128)(2,1)}, bf16[512,2048]{1,0:T(8,128)(2,1)}) async-done(((bf16[512,2048]{1,0:T(8,128)(2,1)}, bf16[512,2048]{1,0:T(8,128)(2,1)}), (bf16[512,2048]{1,0:T(8,128)(2,1)}, bf16[512,2048]{1,0:T(8,128)(2,1)})) %all-reduce.19.cloned.1.call-update) | async-done | bytes 4194320 | tf_op jit(solution)/shard_map/psum | solution.py:201
  1017.6 24.3 %all-reduce.7 = (bf16[2048]{0:T(1024)(128)(2,1)S(1)}, bf16[2048]{0:T(1024)(128)(2,1)S(1)}, bf16[2048]{0:T(1024)(128)(2,1)S(1)}, bf16[2048]{0:T(1024)(128)(2,1)S(...) all-reduce(bf16[2048]{0:T(1024)(128)(2,1)S(1)} %add_convert_fusion., ...), channel_id=2, replica_groups=mesh['dp'=8,'mp'=4] {'dp'}, use_global_device_ids=true, to_apply=%region_32.33.clone | all-reduce | flops 12288 | bytes 49152
  1062.7 18.8 %reduce-scatter.9.cloned.1.call-done = bf16[256,2048]{1,0:T(8,128)(2,1)} async-done(((bf16[2048,2048]{1,0:T(8,128)(2,1)}), bf16[256,2048]{1,0:T(8,128)(2,1)}) %reduce-scatter.9.cloned.1.call-update) | async-done | bytes 1048592 | tf_op jit(solution)/shard_map/reduce_scatter | solution.py:215
  1084.3 72.0 %reduce-scatter.11.cloned.1.call-done = bf16[2048,256]{1,0:T(8,128)(2,1)} async-done(((bf16[2048,2048]{1,0:T(8,128)(2,1)}), bf16[2048,256]{1,0:T(8,128)(2,1)}) %reduce-scatter.11.cloned.1.call-update) | async-done | bytes 1048592 | tf_op jit(solution)/shard_map/reduce_scatter | solution.py:218
  1159.0 62.2 %reduce-scatter.5.cloned.1.call-done = bf16[256,3,512]{2,0,1:T(8,128)(2,1)} async-done(((bf16[2048,3,512]{2,0,1:T(8,128)(2,1)}), bf16[256,3,512]{2,0,1:T(8,128)(2,1)}) %reduce-scatter.5.cloned.1.call-update) | async-done | bytes 786448 | tf_op jit(solution)/shard_map/reduce_scatter | solution.py:209
  (406 shorter events, 215.8 us)
Async XLA Ops:
  7.2 52.6 %all-gather.11.cloned.1.call-start = ((), (), s32[]{:S(2)}) async-start(), calls=%async_computation.4 | async-start | bytes 7077888 | tf_op jit(solution)/shard_map/all_gather | solution.py:64
  9.6 80.3 %all-gather.13.cloned.1.call-start = ((), (), s32[]{:S(2)}) async-start(), calls=%async_computation.5 | async-start | bytes 2359296 | tf_op jit(solution)/shard_map/all_gather | solution.py:65
  10.3 170.0 %all-reduce.15.cloned.1.call-start = ((), (), s32[]{:S(2)}) async-start(), calls=%async_computation.6 | async-start | bytes 4194304 | tf_op jit(solution)/shard_map/psum | solution.py:118
  12.3 54.0 %copy-start.62 = (f32[512]{0:T(512)}, f32[512]{0:T(512)S(1)}, u32[]{:S(2)}) copy-start(f32[512]{0:T(512)S(1)} %broadcast_multiply_fusion.4) | copy-start | bytes 6148
  16.1 50.3 %copy-start.79 = (f32[512]{0:T(512)}, f32[512]{0:T(512)S(1)}, u32[]{:S(2)}) copy-start(f32[512]{0:T(512)S(1)} %fusion.90) | copy-start | bytes 6148
  17.4 753.8 %copy-start.97 = (pred[512]{0:T(512)(128)(4,1)}, pred[512]{0:T(512)(128)(4,1)S(1)}, u32[]{:S(2)}) copy-start(pred[512]{0:T(512)(128)(4,1)S(1)} %iota_compare_fusion.2) | copy-start | bytes 1540
  28.1 156.6 %copy-start.56 = (f32[8,1,256]{2,1,0:T(1,128)}, f32[8,1,256]{2,1,0:T(1,128)S(1)}, u32[]{:S(2)}) copy-start(f32[8,1,256]{2,1,0:T(1,128)S(1)} %convert_element_type.455) | copy-start | bytes 24580
  37.0 147.7 %copy-start.93 = (f32[8,1,256]{2,1,0:T(1,128)}, f32[8,1,256]{2,1,0:T(1,128)S(1)}, u32[]{:S(2)}) copy-start(f32[8,1,256]{2,1,0:T(1,128)S(1)} %convert_element_type.456) | copy-start | bytes 24580
  37.1 154.4 %copy-start.64 = (f32[8,64]{1,0:T(8,128)}, f32[8,64]{1,0:T(8,128)S(1)}, u32[]{:S(2)}) copy-start(f32[8,64]{1,0:T(8,128)S(1)} %add.314) | copy-start | bytes 6148
  37.2 157.8 %copy-start.58 = (f32[8,64]{1,0:T(8,128)}, f32[8,64]{1,0:T(8,128)S(1)}, u32[]{:S(2)}) copy-start(f32[8,64]{1,0:T(8,128)S(1)} %add.311) | copy-start | bytes 6148
  73.6 111.1 %copy-start.39 = (bf16[8,64,512]{2,1,0:T(8,128)(2,1)}, bf16[8,64,512]{2,1,0:T(8,128)(2,1)S(1)}, u32[]{:S(2)}) copy-start(bf16[8,64,512]{2,1,0:T(8,128)(2,1)S(1)} %convolution_convert_fusion.11) | copy-start | bytes 1572868
  94.0 193.1 %all-reduce.17.cloned.1.call-start = ((), (), s32[]{:S(2)}) async-start(), calls=%async_computation.9 | async-start | bytes 4194304 | tf_op jit(solution)/shard_map/psum | solution.py:118
  104.1 646.3 %copy-start.99 = (pred[512]{0:T(512)(128)(4,1)}, pred[512]{0:T(512)(128)(4,1)S(1)}, u32[]{:S(2)}) copy-start(pred[512]{0:T(512)(128)(4,1)S(1)} %iota_compare_fusion.1) | copy-start | bytes 1540
  104.2 87.1 %copy-start.60 = (f32[512]{0:T(512)}, f32[512]{0:T(512)S(1)}, u32[]{:S(2)}) copy-start(f32[512]{0:T(512)S(1)} %broadcast_multiply_fusion.2) | copy-start | bytes 6148
  199.2 88.0 %copy-start.10 = (bf16[512,2048]{1,0:T(8,128)(2,1)S(1)}, bf16[512,2048]{1,0:T(8,128)(2,1)}, u32[]{:S(2)}) copy-start(bf16[512,2048]{1,0:T(8,128)(2,1)} %all-reduce.15.cloned.1.call-done) | copy-start | bytes 6291460
  201.8 140.4 %all-gather.15.cloned.1.call-start = ((), (), s32[]{:S(2)}) async-start(), calls=%async_computation.7 | async-start | bytes 9437184 | tf_op jit(solution)/shard_map/all_gather | solution.py:71
  202.4 197.4 %all-gather.17.cloned.1.call-start = ((), (), s32[]{:S(2)}) async-start(), calls=%async_computation.8 | async-start | bytes 9437184 | tf_op jit(solution)/shard_map/all_gather | solution.py:72
  203.0 547.5 %all-reduce.21.cloned.1.call-start = ((), (), s32[]{:S(2)}) async-start(), calls=%async_computation.15 | async-start | bytes 16777216 | tf_op jit(solution)/shard_map/psum | solution.py:127
  221.0 129.9 %copy-start.95 = (f32[8,1,256]{2,1,0:T(1,128)}, f32[8,1,256]{2,1,0:T(1,128)S(1)}, u32[]{:S(2)}) copy-start(f32[8,1,256]{2,1,0:T(1,128)S(1)} %convert_element_type.459) | copy-start | bytes 24580
  292.9 498.5 %copy-start.71 = (f32[512]{0:T(512)}, f32[512]{0:T(512)S(1)}, u32[]{:S(2)}) copy-start(f32[512]{0:T(512)S(1)} %fusion.93) | copy-start | bytes 6148
  292.9 478.3 %copy-start.73 = (f32[512]{0:T(512)}, f32[512]{0:T(512)S(1)}, u32[]{:S(2)}) copy-start(f32[512]{0:T(512)S(1)} %fusion.91) | copy-start | bytes 6148
  459.4 504.0 %reduce-scatter.7.cloned.1.call-start = ((), (), s32[]{:S(2)}) async-start(), calls=%async_computation.11 | async-start | bytes 2359296 | tf_op jit(solution)/shard_map/reduce_scatter | solution.py:212
  803.4 204.2 %all-reduce.19.cloned.1.call-start = ((), (), s32[]{:S(2)}) async-start(), calls=%async_computation.14 | async-start | bytes 8388608 | tf_op jit(solution)/shard_map/psum | solution.py:201
  853.4 228.0 %reduce-scatter.9.cloned.1.call-start = ((), (), s32[]{:S(2)}) async-start(), calls=%async_computation.12 | async-start | bytes 9437184 | tf_op jit(solution)/shard_map/reduce_scatter | solution.py:215
  883.5 272.8 %reduce-scatter.11.cloned.1.call-start = ((), (), s32[]{:S(2)}) async-start(), calls=%async_computation.13 | async-start | bytes 9437184 | tf_op jit(solution)/shard_map/reduce_scatter | solution.py:218
  906.1 315.1 %reduce-scatter.5.cloned.1.call-start = ((), (), s32[]{:S(2)}) async-start(), calls=%async_computation.10 | async-start | bytes 7077888 | tf_op jit(solution)/shard_map/reduce_scatter | solution.py:209
  924.8 34.3 %copy-start.66 = (f32[2048]{0:T(1024)S(1)}, f32[2048]{0:T(1024)}, u32[]{:S(2)}) copy-start(f32[2048]{0:T(1024)} %get-tuple-element.30) | copy-start | bytes 24580
  924.9 34.3 %copy-start.67 = (f32[2048]{0:T(1024)S(1)}, f32[2048]{0:T(1024)}, u32[]{:S(2)}) copy-start(f32[2048]{0:T(1024)} %get-tuple-element.72) | copy-start | bytes 24580
  924.9 34.3 %copy-start.68 = (f32[2048]{0:T(1024)S(1)}, f32[2048]{0:T(1024)}, u32[]{:S(2)}) copy-start(f32[2048]{0:T(1024)} %get-tuple-element.70) | copy-start | bytes 24580
  924.9 34.3 %copy-start.28 = (bf16[512,2048]{1,0:T(8,128)(2,1)S(1)}, bf16[512,2048]{1,0:T(8,128)(2,1)}, u32[]{:S(2)}) copy-start(bf16[512,2048]{1,0:T(8,128)(2,1)} %get-tuple-element.78) | copy-start | bytes 6291460
  1013.6 32.2 %copy-start.70 = (f32[512]{0:T(512)S(1)}, f32[512]{0:T(512)}, u32[]{:S(2)}) copy-start(f32[512]{0:T(512)} %copy-done.69) | copy-start | bytes 6148
  1013.6 32.2 %copy-start.86 = (f32[512]{0:T(512)S(1)}, f32[512]{0:T(512)}, u32[]{:S(2)}) copy-start(f32[512]{0:T(512)} %copy-done.85) | copy-start | bytes 6148
  (108 other events, 710.0 us)
Sparse Core Ops, SparseCore 0:
  10.5 49.2 all-gather.10
  61.7 28.0 all-gather.12
  94.2 86.1 all-reduce.14
  201.9 85.1 all-reduce.16
  288.9 53.2 all-gather.14
  343.9 55.8 all-gather.16
  459.5 290.8 all-reduce.20
  803.5 40.1 reduce-scatter.6
  853.5 154.0 all-reduce.18
  1010.9 70.5 reduce-scatter.8
  1084.9 71.2 reduce-scatter.10
  1159.5 61.6 reduce-scatter.4
where the time goes:
time: 1240 us; the launch traced here: 1230 us
  waiting for transfers between devices  729 us (59%)
  matrix products  242 us (20%)
  other arithmetic  108 us (9%)
  blocking collectives  105 us (8%)
  local copies, waits for them, and re-layouts  26.2 us (2%)
  between operations  18.9 us (2%)
    psum x1, waiting for transfers between devices, local(): lax.psum(feed_part.astype(jnp.bfloat16), 'mp').astype(jnp.float32)  282 us
    psum x2, waiting for transfers between devices, local(): lax.psum(attention_part.astype(jnp.bfloat16), 'mp').astype(jnp.float32)  142 us
    reduce_scatter x1, waiting for transfers between devices, local(): lax.psum_scatter(acc_reduce.astype(jnp.bfloat16), 'dp', scatter_dimension...  72 us
    reduce_scatter x1, waiting for transfers between devices, local(): lax.psum_scatter(acc_triple.astype(jnp.bfloat16), 'dp', scatter_dimension...  62.2 us
    all_gather x1, waiting for transfers between devices, local(): lax.all_gather(expand_weight, 'dp', axis=0, tiled=True)  49.2 us
    psum x1, waiting for transfers between devices, local(): lax.psum(grad_in_part.astype(jnp.bfloat16), 'mp').astype(jnp.float32)  42.5 us
    dot_general x2, matrix products, local(): jnp.dot(norm_mid, expand_full, preferred_element_type=jnp.float32)  35.1 us
    dot_general x2, matrix products, local(): jnp.dot(norm_mid.T, grad_pre, preferred_element_type=jnp.float32)  29.3 us
  transfers between devices with their start and end apart: 12, of which 11 were waited for; matrix products, arithmetic and copies ran while one was open for 18% of the time, Pallas kernels for 0%

commit v1 on v0

--- a/solution.py
+++ b/solution.py
@@ -1,12 +1,40 @@
+import functools
 import jax
 import jax.numpy as jnp
 from jax import lax
 from jax.sharding import PartitionSpec as P
+from jax.lax import axis_index, axis_size, ppermute
 
 HEADS = 32
 HEAD_DIM = 64
 SLOT = 512
 MICRO = 2
+
+
+def load_ports(s0, mesh_dim):
+    met_up = axis_index(mesh_dim)
+    new = axis_size(mesh_dim)
+    part_next, h_now, after = (new, met_up, s0.shape[0])
+    rows = [(num, (num + 1) % part_next) for num in range(part_next)]
+    table = [(num, (num - 1) % part_next) for num in range(part_next)]
+    extra = jnp.zeros((*s0.shape[:0], part_next * after, *s0.shape[1:]), s0.dtype)
+    formed = part_now = s0
+    carry_out = part_next // 2
+    extra = lax.dynamic_update_slice_in_dim(extra, s0, h_now * after, axis=0)
+    for dd in range(1, carry_out + 1):
+        formed = ppermute(formed, mesh_dim, rows)
+        extra = lax.dynamic_update_slice_in_dim(
+            extra, formed, (h_now - dd) % part_next * after, axis=0
+        )
+        if dd < part_next - carry_out:
+            part_now = ppermute(part_now, mesh_dim, perm=table)
+            extra = lax.dynamic_update_slice_in_dim(
+                extra, part_now, (h_now + dd) % part_next * after, axis=0
+            )
+    return extra
+
+
+detail_the_packet = functools.partial(load_ports, mesh_dim="dp")
 
 
 def layer_norm(values, gain_vec, shift_vec):
@@ -68,7 +96,7 @@
     feed_kept = (
         lax.all_gather(middle_gain, "dp", axis=0, tiled=True),
         lax.all_gather(middle_shift, "dp", axis=0, tiled=True),
-        lax.all_gather(expand_weight, "dp", axis=0, tiled=True),
+        detail_the_packet(expand_weight),
         lax.all_gather(reduce_weight, "dp", axis=1, tiled=True),
         lax.all_gather(reduce_bias, "dp", axis=0, tiled=True),
     )

time: 1240 us -> 1180 us (0.952)
  waiting for transfers between devices: 729 us -> 625 us
  blocking collectives: 105 us -> 129 us
  local copies, waits for them, and re-layouts: 26.2 us -> 43.8 us
    psum x2, waiting for transfers between devices: 142 us -> 68.5 us  [local(): lax.psum(attention_part.astype(jnp.bfloat16), 'mp').astype(jnp.float32)]
    reduce_scatter x1, waiting for transfers between devices: 18.8 us -> 72.2 us  [local(): lax.psum_scatter(acc_expand.astype(jnp.bfloat16), 'dp', scatter_dimension...]
    reduce_scatter x1, waiting for transfers between devices: 72 us -> 18.7 us  [local(): lax.psum_scatter(acc_reduce.astype(jnp.bfloat16), 'dp', scatter_dimension...]
    all_gather x1 -> x0, waiting for transfers between devices: 49.2 us -> none  [local(): lax.all_gather(expand_weight, 'dp', axis=0, tiled=True)]
    ppermute x0 -> x7, waiting for transfers between devices: none -> 36.1 us  [the longest x3 35 us: load_ports(): part_now = ppermute(part_now, mesh_dim, perm=table)]
    all_gather x1, waiting for transfers between devices: 20.4 us -> 3.27 us  [local(): lax.all_gather(reduce_weight, 'dp', axis=1, tiled=True)]
    all_gather x1, blocking collectives: 8.9 us -> 25.6 us  [local(): lax.all_gather(middle_gain, 'dp', axis=0, tiled=True)]
    dynamic_update_slice x0 -> x8, local copies, waits for them, and re-layouts: none -> 13.7 us  [the longest x4 6.8 us: load_ports(): lax.dynamic_update_slice_in_dim(extra, formed, (h_now - dd) % part_next *...]
  transfers between devices with their start and end apart: 12 -> 18, of which waited for: 11 -> 12; matrix products, arithmetic and copies ran while one was open for 18% -> 22% of each run, Pallas kernels for 0% -> 0%
where the time goes in v1:
time: 1180 us; the launch traced here: 1170 us
  waiting for transfers between devices  625 us (53%)
  matrix products  243 us (21%)
  blocking collectives  129 us (11%)
  other arithmetic  109 us (9%)
  local copies, waits for them, and re-layouts  43.8 us (4%)
  between operations  18.7 us (2%)
    psum x1, waiting for transfers between devices, local(): lax.psum(feed_part.astype(jnp.bfloat16), 'mp').astype(jnp.float32)  282 us
    reduce_scatter x1, waiting for transfers between devices, local(): lax.psum_scatter(acc_expand.astype(jnp.bfloat16), 'dp', scatter_dimension...  72.2 us
    psum x2, waiting for transfers between devices, local(): lax.psum(attention_part.astype(jnp.bfloat16), 'mp').astype(jnp.float32)  68.5 us
    reduce_scatter x1, waiting for transfers between devices, local(): lax.psum_scatter(acc_triple.astype(jnp.bfloat16), 'dp', scatter_dimension...  62.3 us
    psum x1, waiting for transfers between devices, local(): lax.psum(grad_in_part.astype(jnp.bfloat16), 'mp').astype(jnp.float32)  42.4 us
    dot_general x2, matrix products, local(): jnp.dot(norm_mid, expand_full, preferred_element_type=jnp.float32)  35.3 us
    ppermute x3, waiting for transfers between devices, load_ports(): part_now = ppermute(part_now, mesh_dim, perm=table)  35 us
    dot_general x2, matrix products, local(): jnp.dot(norm_mid.T, grad_pre, preferred_element_type=jnp.float32)  29.4 us
  transfers between devices with their start and end apart: 18, of which 12 were waited for; matrix products, arithmetic and copies ran while one was open for 22% of the time, Pallas kernels for 0%

profile of v1, /device:TPU:0, one launch (start us, length us, event | category | flops | bytes accessed | tf_op | source)
XLA Modules:
  0.0 1174.5 jit_solution(3290260676207367767)
XLA Ops:
  17.5 10.6 all-gather
  28.1 8.9 all-gather.1
  37.4 22.4 %all-gather.10.cloned.1.call-done = bf16[2048,3,512]{0,2,1:T(8,128)(2,1)} async-done(((bf16[256,3,512]{0,2,1:T(8,128)(2,1)}), bf16[2048,3,512]{0,2,1:T(8,128)(2,1)}) %all-gather.10.cloned.1.call-update) | async-done | bytes 6291472 | tf_op jit(solution)/shard_map/all_gather | solution.py:92
  73.6 16.3 %all-gather.12.cloned.1.call-done = bf16[512,2048]{1,0:T(8,128)(2,1)} async-done(((bf16[512,256]{1,0:T(8,128)(2,1)}), bf16[512,2048]{1,0:T(8,128)(2,1)}) %all-gather.12.cloned.1.call-update) | async-done | bytes 2097168 | tf_op jit(solution)/shard_map/all_gather | solution.py:93
  94.4 16.6 %all-gather.2 = bf16[8,1,256]{2,1,0:T(2,128)(2,1)S(1)} all-gather(bf16[1,1,256]{2,1,0:T(2,128)(2,1)S(1)} %reshape.370), channel_id=1, replica_groups=mesh['dp'=8,'mp'=4] {'dp'}, dimensions={0}, use_global_device_ids=true | all-gather | bytes 4608 | tf_op jit(solution)/shard_map/all_gather | solution.py:94
  111.8 68.5 %all-reduce.15.cloned.1.call-done = bf16[512,2048]{1,0:T(8,128)(2,1)} async-done(((bf16[512,2048]{1,0:T(8,128)(2,1)}), bf16[512,2048]{1,0:T(8,128)(2,1)}) %all-reduce.15.cloned.1.call-update) | async-done | bytes 2097168 | tf_op jit(solution)/shard_map/psum | solution.py:146
  202.9 23.1 %collective-permute-done.1 = bf16[256,2048]{1,0:T(8,128)(2,1)} collective-permute-done((bf16[256,2048]{1,0:T(8,128)(2,1)S(1)}, bf16[256,2048]{1,0:T(8,128)(2,1)}, u32[]{:S(2)}, u32[]{:S(2)}) %collective-permute-start.1) | collective-permute-done | bytes 1048608 | tf_op jit(solution)/shard_map/ppermute | solution.py:30
  229.4 25.6 %all-gather.3 = bf16[8,1,256]{2,1,0:T(2,128)(2,1)S(1)} all-gather(bf16[1,1,256]{2,1,0:T(2,128)(2,1)S(1)} %reshape.372), channel_id=1, replica_groups=mesh['dp'=8,'mp'=4] {'dp'}, dimensions={0}, use_global_device_ids=true | all-gather | bytes 4608 | tf_op jit(solution)/shard_map/all_gather | solution.py:97
  255.0 9.0 all-gather.4
  281.5 11.9 %collective-permute-done.5 = bf16[256,2048]{1,0:T(8,128)(2,1)S(1)} collective-permute-done((bf16[256,2048]{1,0:T(8,128)(2,1)}, bf16[256,2048]{1,0:T(8,128)(2,1)S(1)}, u32[]{:S(2)}, u32[]{:S(2)}) %collective-permute-start.5) | collective-permute-done | bytes 1048608 | tf_op jit(solution)/shard_map/ppermute | solution.py:30
  312.1 27.9 %multiply_convert_fusion.3 = (bf16[512,2048]{1,0:T(8,128)(2,1)}, f32[512,2048]{1,0:T(8,128)}, bf16[512,2048]{1,0:T(8,128)(2,1)}, f32[512,2048]{1,0:T(8,128)}, f32[512,2048]{1,0:T(8,128)}) fusion(f32[2048]{0:T(1024)S(1)} %convert_element_type.369, f32[512,2048]{1,0:T(8,128)S(1)} %fusion.108, bf16[2048,2048]{1,0:T(8,128)(2,1)} %constant_dynamic-update-slice_fusion, ...), kind=kOutput, calls=%fused_computation.120 | convolution fusion | flops 4442816512 | bytes 33591296 | tf_op jit(solution)/shard_map/dot_general | solution.py:152
  343.3 13.2 %convert_reduce_fusion.6 = (f32[2048]{0:T(1024)}, bf16[512,2048]{1,0:T(8,128)(2,1)S(1)}) fusion(f32[512,2048]{1,0:T(8,128)} %get-tuple-element.85, bf16[2048,2048]{1,0:T(8,128)(2,1)} %all-gather.14.cloned.1.call-done, pred[512]{0:T(512)(128)(4,1)S(1)} %iota_compare_fusion.1, bf16[1024,2048]{1,0:T(8,128)(2,1)} %param.16, f32[512,2048]{1,0:T(8,128)} %copy-done.120, ...), kind=kOutput, calls=%fused_computation.81 | convolution fusion | flops 4315936768 | bytes 20988416 | tf_op jit(solution)/shard_map/dot_general | solution.py:174
  356.5 9.9 convolution_convert_fusion
  366.4 11.5 convert_reduce_fusion.7
  377.9 9.9 convolution_convert_fusion.1
  387.9 9.5 convolution_convert_fusion.2
  403.7 8.9 all-gather.5
  412.6 281.5 %all-reduce.21.cloned.1.call-done = (bf16[512,2048]{1,0:T(8,128)(2,1)}, bf16[512,2048]{1,0:T(8,128)(2,1)}, bf16[512,2048]{1,0:T(8,128)(2,1)}, bf16[512,2048]{1,0:T(8,128)(2,1)}) async-done(((bf16[512,2048]{1,0:T(8,128)(2,1)}, bf16[512,2048]{1,0:T(8,128)(2,1)}, bf16[512,2048]{1,0:T(8,128)(2,1)}, bf16[512,2048]{1,0:T(8,128)(2,1)}), (bf16[512,2048]{1,0:T(8,128)(2,1)}, bf16[512,2048]{1,0:T(8,128)(2,1)}, ...) | async-done | bytes 8388624 | tf_op jit(solution)/shard_map/psum | solution.py:155
  694.2 14.7 %select_reduce_fusion.5 = (f32[]{:T(128)}, f32[512]{0:T(512)S(1)}, f32[512]{0:T(512)S(1)}, f32[]{:T(128)}, f32[]{:T(128)}, /*index=5*/f32[]{:T(128)}, f32[]{:T(1...) fusion(bf16[512,2048]{1,0:T(8,128)(2,1)} %get-tuple-element.67,, ...), kind=kLoop, calls=%fused_computation.80 | loop fusion | flops 55567360 | bytes 25224216 | tf_op jit(solution)/shard_map/reduce_sum | solution.py:162
  751.4 9.5 multiply_convert_fusion
  798.8 10.2 fusion.71
  809.0 11.0 add_convert_fusion
  820.7 13.9 %fusion.106 = f32[2048,2048]{1,0:T(8,128)} fusion(bf16[512,2048]{1,0:T(8,128)(2,1)} %copy-done.119, f32[2048]{0:T(1024)S(1)} %bitcast.180, f32[2048]{0:T(1024)S(1)} %bitcast.161, f32[512]{0:T(512)S(1)} %copy-done.74, bf16[512,2048]{1,0:T(8,128)(2,1)} %all-reduce.15.cloned.1.call-done, f32[512]{0:T(512)S(1)} %broadcast_multiply_fusion.3, ...), kind=kOutput, calls=%fused_computation.257 | convolution fusion | flops 4304404480 | bytes 23097344 | tf_op jit(solution)/shard_map/dot_general | solution.py:178
  834.5 15.5 %add_convert_fusion.1 = bf16[2048,2048]{1,0:T(8,128)(2,1)} fusion(f32[2048,2048]{1,0:T(8,128)} %fusion.106, bf16[512,2048]{1,0:T(8,128)(2,1)} %copy-done.121, f32[512]{0:T(512)S(1)} %copy-done.72, f32[2048]{0:T(1024)S(1)} %bitcast.181, f32[2048]{0:T(1024)S(1)} %bitcast.162, bf16[512,2048]{1,0:T(8,128)(2,1)} %all-reduce.17.cloned.1.call-done, ...), kind=kOutput, calls=%fused_computation.1 | convolution fusion | flops 4312793088 | bytes 31485952 | tf_op jit(solution)/shard_map/dot_general | solution.py:178
  851.4 8.6 fusion.70
  860.1 8.6 add_convert_fusion.2
  875.9 25.3 %all-reduce.6 = (f32[2,512]{1,0:T(2,128)}, f32[2048]{0:T(1024)}, f32[4]{0:T(128)S(1)}) all-reduce(f32[2,512]{1,0:T(2,128)S(1)} %maximum_add_fusion, f32[2048]{0:T(1024)S(1)} %add.437, f32[4]{0:T(128)S(1)} %maximum_add_fusion.1), channel_id=1, replica_groups=mesh['dp'=8,'mp'=4] {'dp'}, use_global_device_ids=true, to_apply=%region_41.42 | all-reduce | flops 3076 | bytes 24608 | tf_op jit(solution)/shard_map/psum | solution.py:268
  908.9 42.4 %all-reduce.19.cloned.1.call-done = (bf16[512,2048]{1,0:T(8,128)(2,1)}, bf16[512,2048]{1,0:T(8,128)(2,1)}) async-done(((bf16[512,2048]{1,0:T(8,128)(2,1)}, bf16[512,2048]{1,0:T(8,128)(2,1)}), (bf16[512,2048]{1,0:T(8,128)(2,1)}, bf16[512,2048]{1,0:T(8,128)(2,1)})) %all-reduce.19.cloned.1.call-update) | async-done | bytes 4194320 | tf_op jit(solution)/shard_map/psum | solution.py:229
  961.4 24.3 %all-reduce.7 = (bf16[2048]{0:T(1024)(128)(2,1)S(1)}, bf16[2048]{0:T(1024)(128)(2,1)S(1)}, bf16[2048]{0:T(1024)(128)(2,1)S(1)}, bf16[2048]{0:T(1024)(128)(2,1)S(...) all-reduce(bf16[2048]{0:T(1024)(128)(2,1)S(1)} %add_convert_fusion., ...), channel_id=2, replica_groups=mesh['dp'=8,'mp'=4] {'dp'}, use_global_device_ids=true, to_apply=%region_32.33.clone | all-reduce | flops 12288 | bytes 49152
  1006.5 18.7 %reduce-scatter.11.cloned.1.call-done = bf16[2048,256]{1,0:T(8,128)(2,1)} async-done(((bf16[2048,2048]{1,0:T(8,128)(2,1)}), bf16[2048,256]{1,0:T(8,128)(2,1)}) %reduce-scatter.11.cloned.1.call-update) | async-done | bytes 1048592 | tf_op jit(solution)/shard_map/reduce_scatter | solution.py:246
  1027.9 72.2 %reduce-scatter.9.cloned.1.call-done = bf16[256,2048]{1,0:T(8,128)(2,1)} async-done(((bf16[2048,2048]{1,0:T(8,128)(2,1)}), bf16[256,2048]{1,0:T(8,128)(2,1)}) %reduce-scatter.9.cloned.1.call-update) | async-done | bytes 1048592 | tf_op jit(solution)/shard_map/reduce_scatter | solution.py:243
  1102.9 62.3 %reduce-scatter.5.cloned.1.call-done = bf16[256,3,512]{2,0,1:T(8,128)(2,1)} async-done(((bf16[2048,3,512]{2,0,1:T(8,128)(2,1)}), bf16[256,3,512]{2,0,1:T(8,128)(2,1)}) %reduce-scatter.5.cloned.1.call-update) | async-done | bytes 786448 | tf_op jit(solution)/shard_map/reduce_scatter | solution.py:237
  (426 shorter events, 233.5 us)
Async XLA Ops:
  7.2 52.6 %all-gather.10.cloned.1.call-start = ((), (), s32[]{:S(2)}) async-start(), calls=%async_computation.4 | async-start | bytes 7077888 | tf_op jit(solution)/shard_map/all_gather | solution.py:92
  9.6 80.3 %all-gather.12.cloned.1.call-start = ((), (), s32[]{:S(2)}) async-start(), calls=%async_computation.5 | async-start | bytes 2359296 | tf_op jit(solution)/shard_map/all_gather | solution.py:93
  10.3 170.0 %all-reduce.15.cloned.1.call-start = ((), (), s32[]{:S(2)}) async-start(), calls=%async_computation.6 | async-start | bytes 4194304 | tf_op jit(solution)/shard_map/psum | solution.py:146
  12.3 54.0 %copy-start.62 = (f32[512]{0:T(512)}, f32[512]{0:T(512)S(1)}, u32[]{:S(2)}) copy-start(f32[512]{0:T(512)S(1)} %broadcast_multiply_fusion.4) | copy-start | bytes 6148
  16.1 50.3 %copy-start.79 = (f32[512]{0:T(512)}, f32[512]{0:T(512)S(1)}, u32[]{:S(2)}) copy-start(f32[512]{0:T(512)S(1)} %fusion.90) | copy-start | bytes 6148
  17.4 49.0 %copy-start.97 = (pred[512]{0:T(512)(128)(4,1)}, pred[512]{0:T(512)(128)(4,1)S(1)}, u32[]{:S(2)}) copy-start(pred[512]{0:T(512)(128)(4,1)S(1)} %iota_compare_fusion.2) | copy-start | bytes 1540
  28.1 156.6 %copy-start.56 = (f32[8,1,256]{2,1,0:T(1,128)}, f32[8,1,256]{2,1,0:T(1,128)S(1)}, u32[]{:S(2)}) copy-start(f32[8,1,256]{2,1,0:T(1,128)S(1)} %convert_element_type.455) | copy-start | bytes 24580
  37.0 147.7 %copy-start.93 = (f32[8,1,256]{2,1,0:T(1,128)}, f32[8,1,256]{2,1,0:T(1,128)S(1)}, u32[]{:S(2)}) copy-start(f32[8,1,256]{2,1,0:T(1,128)S(1)} %convert_element_type.456) | copy-start | bytes 24580
  37.1 153.9 %copy-start.64 = (f32[8,64]{1,0:T(8,128)}, f32[8,64]{1,0:T(8,128)S(1)}, u32[]{:S(2)}) copy-start(f32[8,64]{1,0:T(8,128)S(1)} %add.373) | copy-start | bytes 6148
  37.2 157.2 %copy-start.58 = (f32[8,64]{1,0:T(8,128)}, f32[8,64]{1,0:T(8,128)S(1)}, u32[]{:S(2)}) copy-start(f32[8,64]{1,0:T(8,128)S(1)} %add.370) | copy-start | bytes 6148
  73.5 111.1 %copy-start.38 = (bf16[8,64,512]{2,1,0:T(8,128)(2,1)}, bf16[8,64,512]{2,1,0:T(8,128)(2,1)S(1)}, u32[]{:S(2)}) copy-start(bf16[8,64,512]{2,1,0:T(8,128)(2,1)S(1)} %convolution_convert_fusion.11) | copy-start | bytes 1572868
  94.0 202.6 %all-reduce.17.cloned.1.call-start = ((), (), s32[]{:S(2)}) async-start(), calls=%async_computation.8 | async-start | bytes 4194304 | tf_op jit(solution)/shard_map/psum | solution.py:146
  94.1 108.8 %collective-permute-start = (bf16[256,2048]{1,0:T(8,128)(2,1)S(1)}, bf16[256,2048]{1,0:T(8,128)(2,1)S(1)}, u32[]{:S(2)}, u32[]{:S(2)}) collective-permute-start(bf16[256,2048]{1,0:T(8,128)(2,1)S(1)} %copy-done.40), channel_id=1, source_target_pairs={{0,4},{4,8},{8,12},{12,16},{16,20},{20,24},{24,28},{28,0},{1,5},{5... | collective-permute-start | bytes 3145736 | tf_op jit(solution)/shard_map/ppermute | solution.py:25
  111.6 582.5 %copy-start.100 = (pred[512]{0:T(512)(128)(4,1)}, pred[512]{0:T(512)(128)(4,1)S(1)}, u32[]{:S(2)}) copy-start(pred[512]{0:T(512)(128)(4,1)S(1)} %iota_compare_fusion.1) | copy-start | bytes 1540
  111.7 79.0 %copy-start.60 = (f32[512]{0:T(512)}, f32[512]{0:T(512)S(1)}, u32[]{:S(2)}) copy-start(f32[512]{0:T(512)S(1)} %broadcast_multiply_fusion.2) | copy-start | bytes 6148
  198.7 56.3 %copy-start.113 = (bf16[256]{0:T(256)(128)(2,1)S(1)}, bf16[256]{0:T(256)(128)(2,1)}, u32[]{:S(2)}) copy-start(bf16[256]{0:T(256)(128)(2,1)} %param.25) | copy-start | bytes 1540
  198.7 65.3 %copy-start.103 = (bf16[2048]{0:T(1024)(128)(2,1)S(1)}, bf16[2048]{0:T(1024)(128)(2,1)}, u32[]{:S(2)}) copy-start(bf16[2048]{0:T(1024)(128)(2,1)} %param.27) | copy-start | bytes 12292
  201.3 142.0 %all-gather.14.cloned.1.call-start = ((), (), s32[]{:S(2)}) async-start(), calls=%async_computation.7 | async-start | bytes 9437184 | tf_op jit(solution)/shard_map/all_gather | solution.py:100
  201.3 24.6 %collective-permute-start.1 = (bf16[256,2048]{1,0:T(8,128)(2,1)S(1)}, bf16[256,2048]{1,0:T(8,128)(2,1)}, u32[]{:S(2)}, u32[]{:S(2)}) collective-permute-start(bf16[256,2048]{1,0:T(8,128)(2,1)S(1)} %copy-done.40), channel_id=1, source_target_pairs={{0,28},{4,0},{8,4},{12,8},{16,12},{20,16},{24,20},{28,24},{1,29},{... | collective-permute-start | bytes 3145736 | tf_op jit(solution)/shard_map/ppermute | solution.py:30
  202.9 26.3 %collective-permute-start.2 = (bf16[256,2048]{1,0:T(8,128)(2,1)S(1)}, bf16[256,2048]{1,0:T(8,128)(2,1)}, u32[]{:S(2)}, u32[]{:S(2)}) collective-permute-start(bf16[256,2048]{1,0:T(8,128)(2,1)S(1)} %collective-permute-done), channel_id=1, source_target_pairs={{0,4},{4,8},{8,12},{12,16},{16,20},{20,24},{24,28},{28,0},{1,5},{5... | collective-permute-start | bytes 3145736 | tf_op jit(solution)/shard_map/ppermute | solution.py:25
  225.9 43.5 %collective-permute-start.3 = (bf16[256,2048]{1,0:T(8,128)(2,1)}, bf16[256,2048]{1,0:T(8,128)(2,1)}, u32[]{:S(2)}, u32[]{:S(2)}) collective-permute-start(bf16[256,2048]{1,0:T(8,128)(2,1)} %collective-permute-done.1), channel_id=1, source_target_pairs={{0,28},{4,0},{8,4},{12,8},{16,12},{20,16},{24,20},{28,24},{1,29},{... | collective-permute-start | bytes 3145736 | tf_op jit(solution)/shard_map/ppermute | solution.py:30
  229.1 42.7 %collective-permute-start.4 = (bf16[256,2048]{1,0:T(8,128)(2,1)}, bf16[256,2048]{1,0:T(8,128)(2,1)}, u32[]{:S(2)}, u32[]{:S(2)}) collective-permute-start(bf16[256,2048]{1,0:T(8,128)(2,1)} %collective-permute-done.2), channel_id=1, source_target_pairs={{0,4},{4,8},{8,12},{12,16},{16,20},{20,24},{24,28},{28,0},{1,5},{5... | collective-permute-start | bytes 3145736 | tf_op jit(solution)/shard_map/ppermute | solution.py:25
  229.2 465.0 %all-reduce.21.cloned.1.call-start = ((), (), s32[]{:S(2)}) async-start(), calls=%async_computation.14 | async-start | bytes 16777216 | tf_op jit(solution)/shard_map/psum | solution.py:155
  269.5 23.9 %collective-permute-start.5 = (bf16[256,2048]{1,0:T(8,128)(2,1)}, bf16[256,2048]{1,0:T(8,128)(2,1)S(1)}, u32[]{:S(2)}, u32[]{:S(2)}) collective-permute-start(bf16[256,2048]{1,0:T(8,128)(2,1)} %collective-permute-done.3), channel_id=1, source_target_pairs={{0,28},{4,0},{8,4},{12,8},{16,12},{20,16},{24,20},{28,24},{1,29},{... | collective-permute-start | bytes 3145736 | tf_op jit(solution)/shard_map/ppermute | solution.py:30
  271.8 23.7 %collective-permute-start.6 = (bf16[256,2048]{1,0:T(8,128)(2,1)}, bf16[256,2048]{1,0:T(8,128)(2,1)S(1)}, u32[]{:S(2)}, u32[]{:S(2)}) collective-permute-start(bf16[256,2048]{1,0:T(8,128)(2,1)} %collective-permute-done.4), channel_id=1, source_target_pairs={{0,4},{4,8},{8,12},{12,16},{16,20},{20,24},{24,28},{28,0},{1,5},{5... | collective-permute-start | bytes 3145736 | tf_op jit(solution)/shard_map/ppermute | solution.py:25
  302.6 432.6 %copy-start.71 = (f32[512]{0:T(512)}, f32[512]{0:T(512)S(1)}, u32[]{:S(2)}) copy-start(f32[512]{0:T(512)S(1)} %fusion.93) | copy-start | bytes 6148
  302.7 412.3 %copy-start.73 = (f32[512]{0:T(512)}, f32[512]{0:T(512)S(1)}, u32[]{:S(2)}) copy-start(f32[512]{0:T(512)S(1)} %fusion.91) | copy-start | bytes 6148
  403.1 504.1 %reduce-scatter.7.cloned.1.call-start = ((), (), s32[]{:S(2)}) async-start(), calls=%async_computation.10 | async-start | bytes 2359296 | tf_op jit(solution)/shard_map/reduce_scatter | solution.py:240
  747.2 204.2 %all-reduce.19.cloned.1.call-start = ((), (), s32[]{:S(2)}) async-start(), calls=%async_computation.13 | async-start | bytes 8388608 | tf_op jit(solution)/shard_map/psum | solution.py:229
  797.2 228.0 %reduce-scatter.11.cloned.1.call-start = ((), (), s32[]{:S(2)}) async-start(), calls=%async_computation.12 | async-start | bytes 9437184 | tf_op jit(solution)/shard_map/reduce_scatter | solution.py:246
  820.0 280.1 %reduce-scatter.9.cloned.1.call-start = ((), (), s32[]{:S(2)}) async-start(), calls=%async_computation.11 | async-start | bytes 9437184 | tf_op jit(solution)/shard_map/reduce_scatter | solution.py:243
  850.1 315.0 %reduce-scatter.5.cloned.1.call-start = ((), (), s32[]{:S(2)}) async-start(), calls=%async_computation.9 | async-start | bytes 7077888 | tf_op jit(solution)/shard_map/reduce_scatter | solution.py:237
  (114 other events, 983.3 us)
Sparse Core Ops, SparseCore 0:
  10.5 49.2 all-gather.9
  61.7 28.0 all-gather.11
  94.2 86.1 all-reduce.14
  201.4 85.1 all-reduce.16
  288.3 54.8 all-gather.13
  403.2 290.8 all-reduce.20
  747.3 40.0 reduce-scatter.6
  797.3 153.9 all-reduce.18
  954.9 70.3 reduce-scatter.10
  1028.5 71.5 reduce-scatter.8
  1103.4 61.6 reduce-scatter.4
